TPU v7x, 32 devices: a whole 2x2x4 slice. The times are simulated.
32 devices in a mesh: seq: 8 (over z, x), head: 4 (over y, core).
Axes of the slice: x: 2, y: 2, z: 4, core: 2. Of those that a mesh axis runs over, the one named last changes fastest.
Arguments:
- queries: bfloat16 [8192, 2048], P('seq', 'head'), may hold values from -64 to 64
- keys: bfloat16 [8192, 2048], P('seq', 'head'), may hold values from -16 to 16
- values: bfloat16 [8192, 2048], P('seq', 'head'), may hold values from -6 to 6
- span_bounds: int32 [16, 2], replicated, may hold values from 0 to 8192, as said below
- mem_decay: float32 [8, 16], P(None, 'head'), may hold values from 0.01 to 1
- mem_gate: float32 [16], P('head'), may hold values from -2 to 2
- out_weight: bfloat16 [2048, 4096], P('head'), may hold values from -0.125 to 0.125
Outputs:
- mixed: bfloat16 [8192, 4096], P('seq', 'head')
Inputs may be any that keep to these rules, and one draw needn't show every extreme that they name: `span_bounds`: slot k lies in segment k // 2, inside the k % 2-th of 2 equal parts of it; start <= end, an empty slot has start == end; some slot covers a whole part.
All inputs are finite; a program needn't handle non-finite values.
Results may differ from a plain program's by a relative error of at most 0.0052.
The roundings to bfloat16 on the way count: a program that leaves them out, or rounds other values in their place, can miss the bound.
Values may be sent and summed in bfloat16 or wider, within the bound.
No kernel may reach another device: no remote copies, remote signals or barrier semaphores. Data moves between devices by JAX's collectives and lax.ppermute only.
A program may use at most 128 MiB of HBM per device.

v0:
```python
import math
import jax
import jax.numpy as jnp
from jax import lax
from jax.sharding import PartitionSpec as P

BAND = 512
SPAN_DEV = 2
HIGHEST_PRECISION = lax.Precision.HIGHEST


def from_behind(block, axis, distance):
    devices = range(lax.axis_size(axis))
    route = [(i - distance, i) for i in devices if i - distance in devices]
    return lax.ppermute(block, axis, route)


def feature_map(values_in):
    return jnp.where(values_in > 0, values_in + 1.0, jnp.exp(jnp.minimum(values_in, 0.0)))


def local_attention(
    queries_3d, band_keys, band_values, query_labels, key_labels, shard_index, band_width
):
    seg_rows, head_count, head_width = queries_3d.shape
    block_rows = min(seg_rows, 512)
    key_count = band_keys.shape[0]
    key_pos = jnp.arange(key_count) - band_width
    key_valid = (key_pos >= 0) | (shard_index > 0)
    score_scale = 1.0 / math.sqrt(head_width)

    def attend_block(block_index):
        row_start = block_index * block_rows
        query_block = lax.dynamic_slice_in_dim(queries_3d, row_start, block_rows, 0)
        label_block = lax.dynamic_slice_in_dim(query_labels, row_start, block_rows, 0)
        query_pos = row_start + jnp.arange(block_rows)
        scores = (
            jnp.einsum("qhd,khd->hqk", query_block, band_keys, preferred_element_type=jnp.float32)
            * score_scale
        )
        nearby = (
            (key_pos[None, :] <= query_pos[:, None])
            & (key_pos[None, :] > query_pos[:, None] - band_width)
            & key_valid[None, :]
        )
        same_span = (label_block[:, None] > 0) & (label_block[:, None] == key_labels[None, :])
        visible = nearby | same_span
        scores = jnp.where(visible[None], scores, -1e30)
        top_score = jnp.max(scores, axis=-1, keepdims=True)
        weights = jnp.exp(scores - top_score)
        totals = jnp.sum(weights, axis=-1)
        mixed_out = jnp.einsum(
            "hqk,khd->qhd",
            weights.astype(jnp.bfloat16),
            band_values,
            preferred_element_type=jnp.float32,
        )
        return mixed_out / jnp.transpose(totals)[:, :, None]

    blocks = lax.map(attend_block, jnp.arange(seg_rows // block_rows))
    return blocks.reshape(seg_rows, head_count, head_width)


def body(queries, keys, values, span_bounds, mem_decay, mem_gate, out_weight):
    seg_rows = queries.shape[0]
    head_count = mem_gate.shape[0]
    head_width = queries.shape[1] // head_count
    band_width = BAND
    shard_index = lax.axis_index("seq")
    prev_keys, prev_values = from_behind(
        (keys[seg_rows - band_width :], values[seg_rows - band_width :]), "seq", 1
    )
    key_feats = feature_map(keys.astype(jnp.float32)).reshape(seg_rows, head_count, head_width)
    value_rows = values.astype(jnp.float32).reshape(seg_rows, head_count, head_width)
    state = jnp.einsum("thd,the->hde", key_feats, value_rows, precision=HIGHEST_PRECISION)
    feat_sum = jnp.sum(key_feats, axis=0)
    cumulative = jnp.cumsum(jnp.log(mem_decay), axis=0)
    before = lax.dynamic_index_in_dim(
        cumulative, jnp.maximum(shard_index - 1, 0), 0, keepdims=False
    )
    part_state = lax.all_gather(state[None], "seq", axis=0, tiled=True)
    part_sum = lax.all_gather(feat_sum[None], "seq", axis=0, tiled=True)
    piece_count = part_state.shape[0]
    piece_index = jnp.arange(piece_count)
    factor = jnp.where(
        (piece_index < shard_index)[:, None],
        jnp.exp(jnp.minimum(before[None, :] - cumulative, 0.0)),
        0.0,
    )
    memory = jnp.einsum("nh,nhde->hde", factor, part_state, precision=HIGHEST_PRECISION)
    feat_total = jnp.einsum("nh,nhd->hd", factor, part_sum, precision=HIGHEST_PRECISION)
    query_feats = feature_map(queries.astype(jnp.float32)).reshape(seg_rows, head_count, head_width)
    numer = jnp.einsum("thd,hde->the", query_feats, memory, precision=HIGHEST_PRECISION)
    denom = jnp.einsum("thd,hd->th", query_feats, feat_total, precision=HIGHEST_PRECISION) + 1.0
    readout = numer / denom[:, :, None]
    own_spans = lax.dynamic_slice_in_dim(span_bounds, shard_index * SPAN_DEV, SPAN_DEV, 0)
    positions = shard_index * seg_rows + jnp.arange(seg_rows)
    inside = (positions[:, None] >= own_spans[None, :, 0]) & (
        positions[:, None] < own_spans[None, :, 1]
    )
    slot_ids = (jnp.arange(SPAN_DEV) + 1)[None, :]
    query_labels = jnp.sum(inside.astype(jnp.int32) * slot_ids, axis=1)
    key_labels = jnp.concatenate([jnp.zeros((band_width,), jnp.int32), query_labels])
    band_keys = jnp.concatenate([prev_keys, keys], axis=0).reshape(
        band_width + seg_rows, head_count, head_width
    )
    band_values = jnp.concatenate([prev_values, values], axis=0).reshape(
        band_width + seg_rows, head_count, head_width
    )
    queries_3d = queries.reshape(seg_rows, head_count, head_width)
    local = local_attention(
        queries_3d, band_keys, band_values, query_labels, key_labels, shard_index, band_width
    )
    gate = jax.nn.sigmoid(mem_gate)[None, :, None]
    attended = (
        (gate * readout + (1.0 - gate) * local)
        .astype(jnp.bfloat16)
        .reshape(seg_rows, head_count * head_width)
    )
    gathered = lax.all_gather(attended, "head", axis=1, tiled=True)
    columns = lax.all_to_all(out_weight, "head", split_axis=1, concat_axis=0, tiled=True)
    mixed = jnp.dot(gathered, columns, preferred_element_type=jnp.float32)
    return mixed.astype(jnp.bfloat16)


def solution(mesh):
    return jax.shard_map(
        body,
        mesh=mesh,
        in_specs=(
            P("seq", "head"),
            P("seq", "head"),
            P("seq", "head"),
            P(),
            P(None, "head"),
            P("head"),
            P("head", None),
        ),
        out_specs=P("seq", "head"),
        check_vma=False,
    )
```

profile of v0, /device:TPU:0, one launch (start us, length us, event | category | flops | bytes accessed | tf_op | source)
XLA Modules:
  0.0 270.6 jit_solution(7278276117064473592)
XLA Ops:
  6.5 1.6 copy.56
  8.1 0.9 slice.16
  9.0 5.7 %collective-permute-start = (bf16[512,512]{0,1:T(8,128)(2,1)}, bf16[512,512]{0,1:T(8,128)(2,1)}, u32[]{:S(2)}, u32[]{:S(2)}) collective-permute-start(bf16[512,512]{0,1:T(8,128)(2,1)} %slice.16), channel_id=1, source_target_pairs={{0,4},{4,8},{8,12},{12,16},{16,20},{20,24},{24,28},{1,5},{5,9},{9,... | collective-permute-start | bytes 1572872 | tf_op jit(solution)/shard_map/ppermute | solution.py:15
  14.7 0.5 copy.58
  15.3 0.8 slice.17
  16.1 3.5 %collective-permute-start.1 = (bf16[512,512]{0,1:T(8,128)(2,1)}, bf16[512,512]{0,1:T(8,128)(2,1)}, u32[]{:S(2)}, u32[]{:S(2)}) collective-permute-start(bf16[512,512]{0,1:T(8,128)(2,1)} %slice.17), channel_id=1, source_target_pairs={{0,4},{4,8},{8,12},{12,16},{16,20},{20,24},{24,28},{1,5},{5,9},{9,... | collective-permute-start | bytes 1572872 | tf_op jit(solution)/shard_map/ppermute | solution.py:15
  19.6 1.8 fusion.35
  21.4 1.8 copy.75
  23.2 3.8 %fusion.29 = f32[4,128,128]{2,1,0:T(8,128)} fusion(f32[1024,4,128]{0,2,1:T(8,128)} %bitcast.87, bf16[1024,512]{1,0:T(8,128)(2,1)} %param.11), kind=kOutput, calls=%fused_computation.42 | convolution fusion | flops 805306368 | bytes 3407872 | tf_op jit(solution)/shard_map/thd,the->hde/dot_general | solution.py:75
  27.1 0.1 constant_dynamic-slice_fusion
  27.1 37.5 %all_gather.10 = f32[8,4,128]{2,1,0:T(4,128)S(1)} all-gather(f32[1,4,128]{2,1,0:T(4,128)S(1)} %bitcast.97), channel_id=1, replica_groups=mesh['seq'=8,'head'=4] {'seq'}, dimensions={0}, use_global_device_ids=true | all-gather | bytes 18432 | tf_op jit(solution)/shard_map/all_gather | solution.py:82
  64.7 1.8 fusion.22
  66.5 1.9 copy.81
  68.4 0.2 reduce_window_sum.11
  68.6 0.2 dynamic-slice_reduce_fusion
  68.8 0.1 exponential_select_fusion
  68.9 0.2 convolution_bitcast_fusion
  69.0 1.1 fusion.36
  70.1 0.1 fusion.34
  70.3 2.3 copy.55
  72.6 2.6 pad_maximum_fusion
  75.2 1.9 copy.61
  77.2 2.3 pad_maximum_fusion.1
  79.5 2.6 copy.62
  82.1 77.2 %while.14 = (s32[]{:T(128)}, f32[2,512,4,128]{1,0,3,2:T(2,128)}, s32[2]{0:T(128)S(1)}, s32[1024]{0:T(1024)S(1)}, s32[1536]{0:T(1024)S(1)}, /*index=5*/bf16[1024,...) while((s32[]{:T(128)}, f32[2,512,4,128]{1,0,3,2:T(2,128)}, ...), condition=%wide.region_6.7_spmd.clone.clone, body=%wide.region_3.6_spmd.clone.clone.sunk | while | flops 1650986496 | bytes 49885384 | solution.py:60
  82.1 0.6 dynamic_slice.46
  83.3 0.1 broadcast_compare_fusion.2
  83.4 1.4 and_or_fusion.2
  84.9 4.1 %fusion.57 = (f32[4,512]{1,0:T(4,128)S(1)}, f32[4,512,1536]{2,1,0:T(8,128)S(1)}) fusion(pred[512,1536]{1,0:T(8,128)(4,1)S(1)} %and_or_fusion.2, bf16[1536,4,128]{2,0,1:T(8,128)(2,1)S(1)} %get-tuple-element.345, bf16[1024,4,128]{0,2,1:T(8,128)(2,1)} %get-tuple-element.344, s32[]{:T(128)S(6)} %select_n.64), kind=kOutput, calls=%fused_computation.4.clone.1 | convolution fusion | flops 814741504 | bytes 15474692 | tf_op jit(solution)/shard_map/while/body/eval_jaxpr/qhd,khd->hqk/dot_general | solution.py:38
  89.0 3.6 %fusion.58 = f32[4,512]{1,0:T(4,128)S(1)} fusion(f32[4,512,1536]{2,1,0:T(8,128)S(1)} %get-tuple-element.311, f32[4,512]{1,0:T(4,128)S(1)} %get-tuple-element.312, pred[512,1536]{1,0:T(8,128)(4,1)S(1)} %and_or_fusion.2), kind=kLoop, calls=%fused_computation.5.clone.1 | loop fusion | flops 12580864 | bytes 13385728 | tf_op jit(solution)/shard_map/while/body/eval_jaxpr/reduce_sum | solution.py:51
  92.7 6.0 %divide_bitcast_fusion.2 = f32[1,512,4,128]{3,1,2,0:T(8,128)} fusion(bf16[1536,4,128]{2,0,1:T(8,128)(2,1)} %get-tuple-element.346, f32[4,512,1536]{2,1,0:T(8,128)S(1)} %get-tuple-element.311, f32[4,512]{1,0:T(4,128)S(1)} %get-tuple-element.312, pred[512,1536]{1,0:T(8,128)(4,1)S(1)} %and_or_fusion.2, f32[512,4]{0,1:T(4,128)S(1)} %bitcast.94), kind=kOutput, calls=%fused_computation.11.clone.1 | convolution fusion | flops 818151424 | bytes 16007168 | tf_op jit(solution)/shard_map/while/body/eval_jaxpr/hqk,khd->qhd/dot_general | solution.py:52
  98.7 2.4 copy.93
  101.1 19.6 %dynamic_update_slice.10 = f32[2,512,4,128]{1,0,3,2:T(2,128)} dynamic-update-slice(f32[2,512,4,128]{1,0,3,2:T(2,128)} %get-tuple-element.327, f32[1,512,4,128]{1,0,3,2:T(1,128)S(1)} %copy.93, s32[]{:T(128)} %get-tuple-element.326, s32[]{:T(128)} %constant.90.clone.1..sunk, s32[]{:T(128)} %constant.90.clone.1..sunk, s32[]{:T(128)} %constant.90.clone.1..sunk) | dynamic-update-slice | bytes 2097156 | tf_op jit(solution)/shard_map/while/body/jit(dynamic_update_index_in_dim)/dynamic_update_slice | solution.py:60
  120.7 0.6 dynamic_slice.46
  121.9 0.1 broadcast_compare_fusion.2
  122.0 1.4 and_or_fusion.2
  123.5 4.1 %fusion.57 = (f32[4,512]{1,0:T(4,128)S(1)}, f32[4,512,1536]{2,1,0:T(8,128)S(1)}) fusion(pred[512,1536]{1,0:T(8,128)(4,1)S(1)} %and_or_fusion.2, bf16[1536,4,128]{2,0,1:T(8,128)(2,1)S(1)} %get-tuple-element.345, bf16[1024,4,128]{0,2,1:T(8,128)(2,1)} %get-tuple-element.344, s32[]{:T(128)S(6)} %select_n.64), kind=kOutput, calls=%fused_computation.4.clone.1 | convolution fusion | flops 814741504 | bytes 15474692 | tf_op jit(solution)/shard_map/while/body/eval_jaxpr/qhd,khd->hqk/dot_general | solution.py:38
  127.6 3.6 %fusion.58 = f32[4,512]{1,0:T(4,128)S(1)} fusion(f32[4,512,1536]{2,1,0:T(8,128)S(1)} %get-tuple-element.311, f32[4,512]{1,0:T(4,128)S(1)} %get-tuple-element.312, pred[512,1536]{1,0:T(8,128)(4,1)S(1)} %and_or_fusion.2), kind=kLoop, calls=%fused_computation.5.clone.1 | loop fusion | flops 12580864 | bytes 13385728 | tf_op jit(solution)/shard_map/while/body/eval_jaxpr/reduce_sum | solution.py:51
  131.3 6.0 %divide_bitcast_fusion.2 = f32[1,512,4,128]{3,1,2,0:T(8,128)} fusion(bf16[1536,4,128]{2,0,1:T(8,128)(2,1)} %get-tuple-element.346, f32[4,512,1536]{2,1,0:T(8,128)S(1)} %get-tuple-element.311, f32[4,512]{1,0:T(4,128)S(1)} %get-tuple-element.312, pred[512,1536]{1,0:T(8,128)(4,1)S(1)} %and_or_fusion.2, f32[512,4]{0,1:T(4,128)S(1)} %bitcast.94), kind=kOutput, calls=%fused_computation.11.clone.1 | convolution fusion | flops 818151424 | bytes 16007168 | tf_op jit(solution)/shard_map/while/body/eval_jaxpr/hqk,khd->qhd/dot_general | solution.py:52
  137.3 2.4 copy.93
  139.7 19.6 %dynamic_update_slice.10 = f32[2,512,4,128]{1,0,3,2:T(2,128)} dynamic-update-slice(f32[2,512,4,128]{1,0,3,2:T(2,128)} %get-tuple-element.327, f32[1,512,4,128]{1,0,3,2:T(1,128)S(1)} %copy.93, s32[]{:T(128)} %get-tuple-element.326, s32[]{:T(128)} %constant.90.clone.1..sunk, s32[]{:T(128)} %constant.90.clone.1..sunk, s32[]{:T(128)} %constant.90.clone.1..sunk) | dynamic-update-slice | bytes 2097156 | tf_op jit(solution)/shard_map/while/body/jit(dynamic_update_index_in_dim)/dynamic_update_slice | solution.py:60
  159.3 4.0 %reshape.179 = f32[1024,4,128]{0,2,1:T(8,128)} reshape(f32[2,512,4,128]{1,0,3,2:T(2,128)} %get-tuple-element.133) | data formatting | bytes 4194304 | tf_op jit(solution)/shard_map/reshape | solution.py:61
  163.3 4.6 %fusion.27 = f32[4,1,128,128]{3,1,2,0:T(1,128)S(1)} fusion(f32[8,4,1,1]{0,2,3,1:T(1,128)S(1)} %bitcast.96, f32[8,4,128,128]{3,2,1,0:T(8,128)} %bitcast.91), kind=kOutput, calls=%fused_computation.36 | convolution fusion | flops 6291456 | bytes 2359424 | tf_op jit(solution)/shard_map/nh,nhde->hde/dot_general | solution.py:90
  167.9 4.8 %fusion.26 = bf16[1024,4,128]{0,2,1:T(8,128)(2,1)} fusion(f32[1024,4,128]{0,2,1:T(8,128)} %reshape.179, f32[4,128,128]{2,1,0:T(8,128)S(1)} %bitcast.93, f32[1024,4,128]{0,2,1:T(8,128)S(1)} %bitcast.86, f32[4]{0:T(128)S(1)} %get-tuple-element.236, f32[1024,4]{0,1:T(4,128)S(1)} %fusion.32, f32[4]{0:T(128)S(1)} %get-tuple-element.237), kind=kOutput, calls=%fused_computation.35 | convolution fusion | flops 807927808 | bytes 5521440 | tf_op jit(solution)/shard_map/thd,hde->the/dot_general | solution.py:93
  172.7 6.6 %copy.64 = bf16[512,4096]{0,1:T(8,128)(2,1)} copy(bf16[512,4096]{1,0:T(8,128)(2,1)} %param.15) | data formatting | bytes 8388608 | tf_op args[6]
  179.3 68.7 %all_to_all.19 = bf16[512,4,1024]{0,2,1:T(8,128)(2,1)} all-to-all(bf16[512,4,1024]{0,2,1:T(8,128)(2,1)} %bitcast.84), channel_id=1, replica_groups=mesh['seq'=8,'head'=4] {'head'}, dimensions={1} | all-to-all | bytes 8388608 | tf_op jit(solution)/shard_map/all_to_all | solution.py:121
  248.0 6.3 %copy.65 = bf16[4,512,1024]{2,1,0:T(8,128)(2,1)} copy(bf16[4,512,1024]{1,2,0:T(8,128)(2,1)} %bitcast.83) | data formatting | bytes 8388608 | tf_op jit(solution)/shard_map/all_to_all | solution.py:121
  254.3 9.4 %convolution_convert_fusion = bf16[1024,1024]{1,0:T(8,128)(2,1)} fusion(bf16[1024,2048]{0,1:T(8,128)(2,1)} %all-gather.4.cloned.1.call-done, bf16[2048,1024]{1,0:T(8,128)(2,1)} %bitcast.90), kind=kOutput, calls=%fused_computation.38 | convolution fusion | flops 4296015872 | bytes 10485760 | tf_op jit(solution)/shard_map/dot_general | solution.py:122
  (42 shorter events, 0.2 us)
Async XLA Ops:
  6.5 20.5 %copy-start = (s32[16,2]{0,1:T(2,128)S(1)}, s32[16,2]{0,1:T(2,128)}, u32[]{:S(2)}) copy-start(s32[16,2]{0,1:T(2,128)} %param.12) | copy-start | bytes 388
  6.5 8.2 %copy-start.6 = (bf16[1024,512]{1,0:T(8,128)(2,1)S(1)}, bf16[1024,512]{1,0:T(8,128)(2,1)}, u32[]{:S(2)}) copy-start(bf16[1024,512]{1,0:T(8,128)(2,1)} %param.11) | copy-start | bytes 3145732
  6.5 156.8 %all-gather.6.cloned.1.call-start = ((), (), s32[]{:S(2)}) async-start(), calls=%async_computation.2 | async-start | bytes 2359296 | tf_op jit(solution)/shard_map/all_gather | solution.py:81
  8.1 8.0 %copy-start.4 = (bf16[1024,512]{0,1:T(8,128)(2,1)}, bf16[1024,512]{0,1:T(8,128)(2,1)S(1)}, u32[]{:S(2)}) copy-start(bf16[1024,512]{0,1:T(8,128)(2,1)S(1)} %copy.56) | copy-start | bytes 3145732
  9.0 63.6 %collective-permute-start = (bf16[512,512]{0,1:T(8,128)(2,1)}, bf16[512,512]{0,1:T(8,128)(2,1)}, u32[]{:S(2)}, u32[]{:S(2)}) collective-permute-start(bf16[512,512]{0,1:T(8,128)(2,1)} %slice.16), channel_id=1, source_target_pairs={{0,4},{4,8},{8,12},{12,16},{16,20},{20,24},{24,28},{1,5},{5,9},{9,... | collective-permute-start | bytes 1572872 | tf_op jit(solution)/shard_map/ppermute | solution.py:15
  16.1 61.0 %collective-permute-start.1 = (bf16[512,512]{0,1:T(8,128)(2,1)}, bf16[512,512]{0,1:T(8,128)(2,1)}, u32[]{:S(2)}, u32[]{:S(2)}) collective-permute-start(bf16[512,512]{0,1:T(8,128)(2,1)} %slice.17), channel_id=1, source_target_pairs={{0,4},{4,8},{8,12},{12,16},{16,20},{20,24},{24,28},{1,5},{5,9},{9,... | collective-permute-start | bytes 1572872 | tf_op jit(solution)/shard_map/ppermute | solution.py:15
  23.2 4.0 %copy-start.7 = (f32[8,4]{0,1:T(4,128)S(1)}, f32[8,4]{0,1:T(4,128)}, u32[]{:S(2)}) copy-start(f32[8,4]{0,1:T(4,128)} %param.13) | copy-start | bytes 388
  23.2 41.5 %copy-start.5 = (bf16[1024,512]{1,0:T(8,128)(2,1)S(1)}, bf16[1024,512]{1,0:T(8,128)(2,1)}, u32[]{:S(2)}) copy-start(bf16[1024,512]{1,0:T(8,128)(2,1)} %param.9) | copy-start | bytes 3145732
  27.0 227.4 %all-gather.4.cloned.1.call-start = ((), (), s32[]{:S(2)}) async-start(), calls=%async_computation.1 | async-start | bytes 5242880 | tf_op jit(solution)/shard_map/all_gather | solution.py:120
  68.4 4.2 %copy-start.2 = (f32[1024,512]{0,1:T(8,128)}, f32[1024,512]{0,1:T(8,128)S(1)}, u32[]{:S(2)}) copy-start(f32[1024,512]{0,1:T(8,128)S(1)} %copy.81) | copy-start | bytes 6291460
  68.4 1.7 copy-start.8
  163.3 4.6 %copy-start.3 = (f32[1024,512]{0,1:T(8,128)S(1)}, f32[1024,512]{0,1:T(8,128)}, u32[]{:S(2)}) copy-start(f32[1024,512]{0,1:T(8,128)} %copy-done.2) | copy-start | bytes 6291460
  254.3 9.4 %copy-start.1 = (s32[16,2]{0,1:T(2,128)S(1)}, s32[16,2]{0,1:T(2,128)}, u32[]{:S(2)}) copy-start(s32[16,2]{0,1:T(2,128)} %param.12) | copy-start | bytes 388
Sparse Core Ops, SparseCore 0:
  27.1 49.7 all-gather.5
  172.8 46.6 all-gather.3
where the time goes:
time: 274 us; the launch traced here: 271 us
  blocking collectives  106 us (39%)
  local copies, waits for them, and re-layouts  76.8 us (28%)
  matrix products  44 us (16%)
  other arithmetic  19.3 us (7%)
  between operations  13.6 us (5%)
  starting transfers between devices  9.21 us (3%)
    all_to_all x1, blocking collectives, body(): lax.all_to_all(out_weight, 'head', split_axis=1, concat_axis=0, tiled=True)  68.7 us
    dynamic_update_slice x4, local copies, waits for them, and re-layouts, local_attention(): blocks = lax.map(attend_block, jnp.arange(seg_rows // block_rows))  44 us
    all_gather x1, blocking collectives, body(): part_sum = lax.all_gather(feat_sum[None], 'seq', axis=0, tiled=True)  37.5 us
    unnamed x24, local copies, waits for them, and re-layouts  15.5 us
    dot_general x2, matrix products, attend_block(): jnp.einsum('hqk,khd->qhd', weights.astype(jnp.bfloat16), band_values, pre...  12 us
    dot_general x1, matrix products, body(): mixed = jnp.dot(gathered, columns, preferred_element_type=jnp.float32)  9.37 us
    ppermute x2, starting transfers between devices, from_behind(): return lax.ppermute(block, axis, route)  9.17 us
    dot_general x2, matrix products, attend_block(): jnp.einsum('qhd,khd->hqk', query_block, band_keys, preferred_element_type...  8.27 us
  transfers between devices with their start and end apart: 4, of which 0 were waited for; matrix products, arithmetic and copies ran while one was open for 44% of the time, Pallas kernels for 0%

commit v1 on v0

--- a/solution.py
+++ b/solution.py
@@ -118,7 +118,10 @@
         .reshape(seg_rows, head_count * head_width)
     )
     gathered = lax.all_gather(attended, "head", axis=1, tiled=True)
-    columns = lax.all_to_all(out_weight, "head", split_axis=1, concat_axis=0, tiled=True)
+    tmp = lax.axis_size("head")
+    everything = jnp.stack(jnp.split(out_weight, tmp, axis=1))
+    after = lax.all_to_all(everything, "head", 0, 0)
+    columns = jnp.concatenate(after, axis=0)
     mixed = jnp.dot(gathered, columns, preferred_element_type=jnp.float32)
     return mixed.astype(jnp.bfloat16)
 

time: 274 us -> 265 us (0.967)
  local copies, waits for them, and re-layouts: 76.8 us -> 66.8 us
  blocking collectives: 106 us -> 110 us
    all_to_all x1 -> x0, local copies, waits for them, and re-layouts: 6.34 us -> none  [body(): lax.all_to_all(out_weight, 'head', split_axis=1, concat_axis=0, tiled=True)]
    unnamed x24 -> x23, local copies, waits for them, and re-layouts: 15.5 us -> 9.2 us
    all_to_all x1, blocking collectives: 68.7 us -> 72.1 us  [body(): after = lax.all_to_all(everything, 'head', 0, 0)]
  transfers between devices with their start and end apart: 4 -> 4, of which waited for: 0 -> 0; matrix products, arithmetic and copies ran while one was open for 44% -> 41% of each run, Pallas kernels for 0% -> 0%
where the time goes in v1:
time: 265 us; the launch traced here: 262 us
  blocking collectives  110 us (42%)
  local copies, waits for them, and re-layouts  66.8 us (25%)
  matrix products  41.7 us (16%)
  other arithmetic  19.8 us (7%)
  between operations  13.6 us (5%)
  starting transfers between devices  9.21 us (3%)
    all_to_all x1, blocking collectives, body(): after = lax.all_to_all(everything, 'head', 0, 0)  72.1 us
    dynamic_update_slice x4, local copies, waits for them, and re-layouts, local_attention(): blocks = lax.map(attend_block, jnp.arange(seg_rows // block_rows))  44 us
    all_gather x1, blocking collectives, body(): part_sum = lax.all_gather(feat_sum[None], 'seq', axis=0, tiled=True)  37.5 us
    dot_general x2, matrix products, attend_block(): jnp.einsum('hqk,khd->qhd', weights.astype(jnp.bfloat16), band_values, pre...  9.72 us
    dot_general x1, matrix products, body(): mixed = jnp.dot(gathered, columns, preferred_element_type=jnp.float32)  9.37 us
    unnamed x23, local copies, waits for them, and re-layouts  9.2 us
    ppermute x2, starting transfers between devices, from_behind(): return lax.ppermute(block, axis, route)  9.17 us
    dot_general x2, matrix products, attend_block(): jnp.einsum('qhd,khd->hqk', query_block, band_keys, preferred_element_type...  8.27 us
  transfers between devices with their start and end apart: 4, of which 0 were waited for; matrix products, arithmetic and copies ran while one was open for 41% of the time, Pallas kernels for 0%

profile of v1, /device:TPU:0, one launch (start us, length us, event | category | flops | bytes accessed | tf_op | source)
XLA Modules:
  0.0 262.2 jit_solution(17488332635209979934)
XLA Ops:
  6.5 1.6 copy.40
  8.1 0.9 slice.16
  9.0 0.2 copy-done.4
  9.3 5.7 %collective-permute-start = (bf16[512,512]{0,1:T(8,128)(2,1)}, bf16[512,512]{0,1:T(8,128)(2,1)}, u32[]{:S(2)}, u32[]{:S(2)}) collective-permute-start(bf16[512,512]{0,1:T(8,128)(2,1)} %slice.16), channel_id=1, source_target_pairs={{0,4},{4,8},{8,12},{12,16},{16,20},{20,24},{24,28},{1,5},{5,9},{9,... | collective-permute-start | bytes 1572872 | tf_op jit(solution)/shard_map/ppermute | solution.py:15
  15.0 0.5 copy.42
  15.5 0.8 slice.17
  16.4 3.5 %collective-permute-start.1 = (bf16[512,512]{0,1:T(8,128)(2,1)}, bf16[512,512]{0,1:T(8,128)(2,1)}, u32[]{:S(2)}, u32[]{:S(2)}) collective-permute-start(bf16[512,512]{0,1:T(8,128)(2,1)} %slice.17), channel_id=1, source_target_pairs={{0,4},{4,8},{8,12},{12,16},{16,20},{20,24},{24,28},{1,5},{5,9},{9,... | collective-permute-start | bytes 1572872 | tf_op jit(solution)/shard_map/ppermute | solution.py:15
  19.8 1.8 fusion.35
  21.6 1.8 copy.57
  23.4 3.8 %fusion.29 = f32[4,128,128]{2,1,0:T(8,128)} fusion(f32[1024,4,128]{0,2,1:T(8,128)} %bitcast.91, bf16[1024,512]{1,0:T(8,128)(2,1)} %param.11), kind=kOutput, calls=%fused_computation.43 | convolution fusion | flops 805306368 | bytes 3407872 | tf_op jit(solution)/shard_map/thd,the->hde/dot_general | solution.py:75
  27.4 37.5 %all_gather.10 = f32[8,4,128]{2,1,0:T(4,128)S(1)} all-gather(f32[1,4,128]{2,1,0:T(4,128)S(1)} %bitcast.101), channel_id=1, replica_groups=mesh['seq'=8,'head'=4] {'seq'}, dimensions={0}, use_global_device_ids=true | all-gather | bytes 18432 | tf_op jit(solution)/shard_map/all_gather | solution.py:82
  64.9 1.8 fusion.22
  66.7 1.9 copy.63
  68.6 0.2 reduce_window_sum.11
  68.8 0.2 dynamic-slice_reduce_fusion
  69.0 0.1 exponential_select_fusion
  69.1 0.2 convolution_bitcast_fusion
  69.3 1.1 fusion.36
  70.4 0.1 fusion.34
  70.5 2.3 copy.39
  72.8 2.6 %pad_maximum_fusion.1 = bf16[1536,512]{0,1:T(8,128)(2,1)} fusion(bf16[1024,512]{0,1:T(8,128)(2,1)} %copy-done.4, bf16[512,512]{0,1:T(8,128)(2,1)} %collective-permute-done), kind=kLoop, calls=%fused_computation.40 | loop fusion | flops 3145728 | bytes 3145728 | tf_op jit(solution)/shard_map/concatenate | solution.py:104
  75.5 1.9 copy.45
  77.4 2.3 pad_maximum_fusion.2
  79.7 2.6 copy.46
  82.3 74.9 %while.14 = (s32[]{:T(128)}, f32[2,512,4,128]{1,0,3,2:T(2,128)}, s32[2]{0:T(128)S(1)}, s32[1024]{0:T(1024)S(1)}, s32[1536]{0:T(1024)S(1)}, /*index=5*/bf16[1024,...) while((s32[]{:T(128)}, f32[2,512,4,128]{1,0,3,2:T(2,128)}, ...), condition=%wide.region_6.7_spmd.clone.clone, body=%wide.region_3.6_spmd.clone.clone.sunk | while | flops 1650986496 | bytes 56176868 | solution.py:60
  82.3 0.6 dynamic_slice.46
  83.6 0.1 broadcast_compare_fusion.2
  83.7 1.4 and_or_fusion.2
  85.1 4.1 %fusion.57 = (f32[4,512]{1,0:T(4,128)S(1)}, f32[4,512,1536]{2,1,0:T(8,128)S(1)}) fusion(pred[512,1536]{1,0:T(8,128)(4,1)S(1)} %and_or_fusion.2, bf16[1536,4,128]{2,0,1:T(8,128)(2,1)S(1)} %get-tuple-element.340, bf16[1024,4,128]{0,2,1:T(8,128)(2,1)} %get-tuple-element.339, s32[]{:T(128)S(6)} %select_n.64), kind=kOutput, calls=%fused_computation.4.clone.1 | convolution fusion | flops 814741504 | bytes 15474692 | tf_op jit(solution)/shard_map/while/body/eval_jaxpr/qhd,khd->hqk/dot_general | solution.py:38
  89.3 3.6 %fusion.58 = f32[4,512]{1,0:T(4,128)S(1)} fusion(f32[4,512,1536]{2,1,0:T(8,128)S(1)} %get-tuple-element.306, f32[4,512]{1,0:T(4,128)S(1)} %get-tuple-element.307, pred[512,1536]{1,0:T(8,128)(4,1)S(1)} %and_or_fusion.2), kind=kLoop, calls=%fused_computation.5.clone.1 | loop fusion | flops 12580864 | bytes 13385728 | tf_op jit(solution)/shard_map/while/body/eval_jaxpr/reduce_sum | solution.py:51
  92.9 4.9 %divide_bitcast_fusion.2 = f32[1,512,4,128]{3,1,2,0:T(8,128)} fusion(bf16[1536,4,128]{2,0,1:T(8,128)(2,1)S(1)} %copy-done.7, f32[4,512,1536]{2,1,0:T(8,128)S(1)} %get-tuple-element.306, f32[4,512]{1,0:T(4,128)S(1)} %get-tuple-element.307, pred[512,1536]{1,0:T(8,128)(4,1)S(1)} %and_or_fusion.2, f32[512,4]{0,1:T(4,128)S(1)} %bitcast.98), kind=kOutput, calls=%fused_computation.11.clone.1 | convolution fusion | flops 818151424 | bytes 16007168 | tf_op jit(solution)/shard_map/while/body/eval_jaxpr/hqk,khd->qhd/dot_general | solution.py:52
  97.8 2.4 copy.75
  100.2 19.6 %dynamic_update_slice.10 = f32[2,512,4,128]{1,0,3,2:T(2,128)} dynamic-update-slice(f32[2,512,4,128]{1,0,3,2:T(2,128)} %get-tuple-element.322, f32[1,512,4,128]{1,0,3,2:T(1,128)S(1)} %copy.75, s32[]{:T(128)} %get-tuple-element.321, s32[]{:T(128)} %constant.90.clone.1..sunk, s32[]{:T(128)} %constant.90.clone.1..sunk, s32[]{:T(128)} %constant.90.clone.1..sunk) | dynamic-update-slice | bytes 2097156 | tf_op jit(solution)/shard_map/while/body/jit(dynamic_update_index_in_dim)/dynamic_update_slice | solution.py:60
  119.8 0.6 dynamic_slice.46
  121.0 0.1 broadcast_compare_fusion.2
  121.2 1.4 and_or_fusion.2
  122.6 4.1 %fusion.57 = (f32[4,512]{1,0:T(4,128)S(1)}, f32[4,512,1536]{2,1,0:T(8,128)S(1)}) fusion(pred[512,1536]{1,0:T(8,128)(4,1)S(1)} %and_or_fusion.2, bf16[1536,4,128]{2,0,1:T(8,128)(2,1)S(1)} %get-tuple-element.340, bf16[1024,4,128]{0,2,1:T(8,128)(2,1)} %get-tuple-element.339, s32[]{:T(128)S(6)} %select_n.64), kind=kOutput, calls=%fused_computation.4.clone.1 | convolution fusion | flops 814741504 | bytes 15474692 | tf_op jit(solution)/shard_map/while/body/eval_jaxpr/qhd,khd->hqk/dot_general | solution.py:38
  126.7 3.6 %fusion.58 = f32[4,512]{1,0:T(4,128)S(1)} fusion(f32[4,512,1536]{2,1,0:T(8,128)S(1)} %get-tuple-element.306, f32[4,512]{1,0:T(4,128)S(1)} %get-tuple-element.307, pred[512,1536]{1,0:T(8,128)(4,1)S(1)} %and_or_fusion.2), kind=kLoop, calls=%fused_computation.5.clone.1 | loop fusion | flops 12580864 | bytes 13385728 | tf_op jit(solution)/shard_map/while/body/eval_jaxpr/reduce_sum | solution.py:51
  130.4 4.9 %divide_bitcast_fusion.2 = f32[1,512,4,128]{3,1,2,0:T(8,128)} fusion(bf16[1536,4,128]{2,0,1:T(8,128)(2,1)S(1)} %copy-done.7, f32[4,512,1536]{2,1,0:T(8,128)S(1)} %get-tuple-element.306, f32[4,512]{1,0:T(4,128)S(1)} %get-tuple-element.307, pred[512,1536]{1,0:T(8,128)(4,1)S(1)} %and_or_fusion.2, f32[512,4]{0,1:T(4,128)S(1)} %bitcast.98), kind=kOutput, calls=%fused_computation.11.clone.1 | convolution fusion | flops 818151424 | bytes 16007168 | tf_op jit(solution)/shard_map/while/body/eval_jaxpr/hqk,khd->qhd/dot_general | solution.py:52
  135.3 2.4 copy.75
  137.7 19.6 %dynamic_update_slice.10 = f32[2,512,4,128]{1,0,3,2:T(2,128)} dynamic-update-slice(f32[2,512,4,128]{1,0,3,2:T(2,128)} %get-tuple-element.322, f32[1,512,4,128]{1,0,3,2:T(1,128)S(1)} %copy.75, s32[]{:T(128)} %get-tuple-element.321, s32[]{:T(128)} %constant.90.clone.1..sunk, s32[]{:T(128)} %constant.90.clone.1..sunk, s32[]{:T(128)} %constant.90.clone.1..sunk) | dynamic-update-slice | bytes 2097156 | tf_op jit(solution)/shard_map/while/body/jit(dynamic_update_index_in_dim)/dynamic_update_slice | solution.py:60
  157.3 4.0 %reshape.179 = f32[1024,4,128]{0,2,1:T(8,128)} reshape(f32[2,512,4,128]{1,0,3,2:T(2,128)} %get-tuple-element.133) | data formatting | bytes 4194304 | tf_op jit(solution)/shard_map/reshape | solution.py:61
  161.3 4.6 %fusion.27 = f32[4,1,128,128]{3,1,2,0:T(1,128)S(1)} fusion(f32[8,4,1,1]{0,2,3,1:T(1,128)S(1)} %bitcast.100, f32[8,4,128,128]{3,2,1,0:T(8,128)} %bitcast.95), kind=kOutput, calls=%fused_computation.37 | convolution fusion | flops 6291456 | bytes 2359424 | tf_op jit(solution)/shard_map/nh,nhde->hde/dot_general | solution.py:90
  165.9 4.8 %fusion.26 = bf16[1024,4,128]{0,2,1:T(8,128)(2,1)} fusion(f32[1024,4,128]{0,2,1:T(8,128)} %reshape.179, f32[4,128,128]{2,1,0:T(8,128)S(1)} %bitcast.97, f32[1024,4,128]{0,2,1:T(8,128)S(1)} %bitcast.90, f32[4]{0:T(128)S(1)} %get-tuple-element.227, f32[1024,4]{0,1:T(4,128)S(1)} %fusion.32, f32[4]{0:T(128)S(1)} %get-tuple-element.228), kind=kOutput, calls=%fused_computation.36 | convolution fusion | flops 807927808 | bytes 5521440 | tf_op jit(solution)/shard_map/thd,hde->the/dot_general | solution.py:93
  170.7 2.6 %slice_bitcast_fusion.3 = (bf16[1,512,1024]{2,1,0:T(8,128)(2,1)S(1)}, bf16[1,512,1024]{2,1,0:T(8,128)(2,1)S(1)}, bf16[1,512,1024]{2,1,0:T(8,128)(2,1)S(1)}, bf16[1,512,1024]{2,1,0:T(8,128)(2,1)S(1)}) fusion(bf16[512,4096]{1,0:T(8,128)(2,1)} %param.15), kind=kLoop, calls=%fused_computation.49 | loop fusion | bytes 8388608 | tf_op jit(solution)/shard_map/stack | solution.py:122
  173.3 0.6 pad_maximum_fusion
  173.9 72.1 %all_to_all.5 = bf16[4,512,1024]{2,1,0:T(8,128)(2,1)} all-to-all(bf16[4,512,1024]{2,1,0:T(8,128)(2,1)S(1)} %pad_maximum_fusion), channel_id=1, replica_groups=mesh['seq'=8,'head'=4] {'head'}, dimensions={0} | all-to-all | bytes 8388608 | tf_op jit(solution)/shard_map/all_to_all | solution.py:123
  246.0 9.4 %convolution_convert_fusion = bf16[1024,1024]{1,0:T(8,128)(2,1)} fusion(bf16[1024,2048]{0,1:T(8,128)(2,1)} %all-gather.4.cloned.1.call-done, bf16[2048,1024]{1,0:T(8,128)(2,1)} %bitcast.94), kind=kOutput, calls=%fused_computation.39 | convolution fusion | flops 4296015872 | bytes 10485760 | tf_op jit(solution)/shard_map/dot_general | solution.py:125
  (46 shorter events, 0.3 us)
Async XLA Ops:
  6.5 20.7 %copy-start = (s32[16,2]{0,1:T(2,128)S(1)}, s32[16,2]{0,1:T(2,128)}, u32[]{:S(2)}) copy-start(s32[16,2]{0,1:T(2,128)} %param.12) | copy-start | bytes 388
  6.5 8.4 %copy-start.6 = (bf16[1024,512]{1,0:T(8,128)(2,1)S(1)}, bf16[1024,512]{1,0:T(8,128)(2,1)}, u32[]{:S(2)}) copy-start(bf16[1024,512]{1,0:T(8,128)(2,1)} %param.11) | copy-start | bytes 3145732
  6.5 154.8 %all-gather.6.cloned.1.call-start = ((), (), s32[]{:S(2)}) async-start(), calls=%async_computation.2 | async-start | bytes 2359296 | tf_op jit(solution)/shard_map/all_gather | solution.py:81
  8.1 1.1 copy-start.4
  9.3 63.6 %collective-permute-start = (bf16[512,512]{0,1:T(8,128)(2,1)}, bf16[512,512]{0,1:T(8,128)(2,1)}, u32[]{:S(2)}, u32[]{:S(2)}) collective-permute-start(bf16[512,512]{0,1:T(8,128)(2,1)} %slice.16), channel_id=1, source_target_pairs={{0,4},{4,8},{8,12},{12,16},{16,20},{20,24},{24,28},{1,5},{5,9},{9,... | collective-permute-start | bytes 1572872 | tf_op jit(solution)/shard_map/ppermute | solution.py:15
  16.4 61.0 %collective-permute-start.1 = (bf16[512,512]{0,1:T(8,128)(2,1)}, bf16[512,512]{0,1:T(8,128)(2,1)}, u32[]{:S(2)}, u32[]{:S(2)}) collective-permute-start(bf16[512,512]{0,1:T(8,128)(2,1)} %slice.17), channel_id=1, source_target_pairs={{0,4},{4,8},{8,12},{12,16},{16,20},{20,24},{24,28},{1,5},{5,9},{9,... | collective-permute-start | bytes 1572872 | tf_op jit(solution)/shard_map/ppermute | solution.py:15
  23.4 4.0 %copy-start.8 = (f32[8,4]{0,1:T(4,128)S(1)}, f32[8,4]{0,1:T(4,128)}, u32[]{:S(2)}) copy-start(f32[8,4]{0,1:T(4,128)} %param.13) | copy-start | bytes 388
  23.4 41.5 %copy-start.5 = (bf16[1024,512]{1,0:T(8,128)(2,1)S(1)}, bf16[1024,512]{1,0:T(8,128)(2,1)}, u32[]{:S(2)}) copy-start(bf16[1024,512]{1,0:T(8,128)(2,1)} %param.9) | copy-start | bytes 3145732
  27.2 218.8 %all-gather.4.cloned.1.call-start = ((), (), s32[]{:S(2)}) async-start(), calls=%async_computation.1 | async-start | bytes 5242880 | tf_op jit(solution)/shard_map/all_gather | solution.py:120
  68.6 4.2 %copy-start.2 = (f32[1024,512]{0,1:T(8,128)}, f32[1024,512]{0,1:T(8,128)S(1)}, u32[]{:S(2)}) copy-start(f32[1024,512]{0,1:T(8,128)S(1)} %copy.63) | copy-start | bytes 6291460
  68.6 1.7 copy-start.9
  89.3 3.7 %copy-start.7 = (bf16[1536,4,128]{2,0,1:T(8,128)(2,1)S(1)}, bf16[1536,4,128]{2,0,1:T(8,128)(2,1)}, u32[]{:S(2)}) copy-start(bf16[1536,4,128]{2,0,1:T(8,128)(2,1)} %get-tuple-element.341) | copy-start | bytes 4718596 | tf_op jit(solution)/shard_map/while
  126.7 3.7 %copy-start.7 = (bf16[1536,4,128]{2,0,1:T(8,128)(2,1)S(1)}, bf16[1536,4,128]{2,0,1:T(8,128)(2,1)}, u32[]{:S(2)}) copy-start(bf16[1536,4,128]{2,0,1:T(8,128)(2,1)} %get-tuple-element.341) | copy-start | bytes 4718596 | tf_op jit(solution)/shard_map/while
  161.3 4.6 %copy-start.3 = (f32[1024,512]{0,1:T(8,128)S(1)}, f32[1024,512]{0,1:T(8,128)}, u32[]{:S(2)}) copy-start(f32[1024,512]{0,1:T(8,128)} %copy-done.2) | copy-start | bytes 6291460
  246.0 9.4 %copy-start.1 = (s32[16,2]{0,1:T(2,128)S(1)}, s32[16,2]{0,1:T(2,128)}, u32[]{:S(2)}) copy-start(s32[16,2]{0,1:T(2,128)} %param.12) | copy-start | bytes 388
Sparse Core Ops, SparseCore 0:
  27.3 49.7 all-gather.5
  170.8 52.3 all-gather.3
